TPU v7x, 32 devices: a whole 2x2x4 slice. The times are simulated.
32 devices in a mesh: dp: 4 (over x, core), vocab: 8 (over z, y).
Axes of the slice: x: 2, y: 2, z: 4, core: 2. Of those that a mesh axis runs over, the one named last changes fastest.
Arguments:
- hidden: bfloat16 [512, 8192], P('dp'), may hold values from -600 to 600
- out_weight: bfloat16 [8192, 98304], P('dp', 'vocab'), may hold values from -0.5 to 0.5
- targets: int32 [512], P('dp'), may hold values from 0 to 98303
- segment: int32 [512], P('dp'), may hold values from 0 to 15, never falling along the last dimension, each value on 1 to 64 neighbouring positions
- loss_mask: int32 [512], P('dp'), may hold values 0 or 1
- outside_count: int32 [16], replicated, may hold values from 0 to 3
Outputs:
- token_loss: float32 [512], P('dp')
- sample_loss: float32 [16], replicated
All inputs are finite; a program needn't handle non-finite values. No bound on the sum of `loss_mask` on one device may be relied on, other than what follows from the above.
Results may differ from a plain program's by a relative error of at most 0.0003.
Values may be sent and summed in bfloat16 or wider, within the bound.
A program may use at most 128 MiB of HBM per device.

v0:
```python
import jax
import jax.numpy as jnp
from jax import lax
from jax.sharding import PartitionSpec as P


def sample_terms(losses, seg_ids, mask_ids, samples):
    onehot = (seg_ids[:, None] == jnp.arange(samples, dtype=jnp.int32)[None, :]).astype(jnp.float32)
    weights = mask_ids.astype(jnp.float32)
    loss_sum = jnp.dot(losses * weights, onehot, precision=lax.Precision.HIGHEST)
    count = jnp.dot(weights, onehot, precision=lax.Precision.HIGHEST)
    return (loss_sum, count)


def body(hidden, out_weight, targets, segment, loss_mask, outside_count):
    shard_cols = out_weight.shape[1]
    samples = outside_count.shape[0]
    vocab_base = lax.axis_index("vocab") * shard_cols
    mixed = lax.all_to_all(hidden, "dp", split_axis=1, concat_axis=0, tiled=True)
    logits = lax.psum_scatter(
        jnp.dot(mixed, out_weight, preferred_element_type=jnp.float32),
        "dp",
        scatter_dimension=0,
        tiled=True,
    )
    local_max = jnp.max(logits, axis=1)
    sumexp = jnp.sum(jnp.exp(logits - local_max[:, None]), axis=1)
    column_ids = jnp.arange(shard_cols, dtype=jnp.int32)[None, :] + vocab_base
    picked = jnp.sum(jnp.where(column_ids == targets[:, None], logits, 0.0), axis=1)
    largest = lax.pmax(local_max, "vocab")
    total, target_logit = lax.psum((sumexp * jnp.exp(local_max - largest), picked), "vocab")
    own_loss = largest + jnp.log(total) - target_logit
    loss_sum, count = sample_terms(own_loss, segment, loss_mask, samples)
    loss_sum, count = lax.psum((loss_sum, count), "dp")
    denom = jnp.maximum(count + outside_count.astype(jnp.float32), 1.0)
    return (own_loss, loss_sum / denom)


def solution(mesh):
    return jax.shard_map(
        body,
        mesh=mesh,
        in_specs=(P("dp", None), P("dp", "vocab"), P("dp"), P("dp"), P("dp"), P()),
        out_specs=(P("dp"), P()),
        check_vma=False,
    )
```

profile of v0, /device:TPU:0, one launch (start us, length us, event | category | flops | bytes accessed | tf_op | source)
XLA Modules:
  0.0 323.0 jit_solution(6669940783405786391)
XLA Ops:
  7.2 0.0 reduce-scatter.2.cloned.1.call-start
  7.2 4.1 %copy.8 = bf16[128,8192]{0,1:T(8,128)(2,1)} copy(bf16[128,8192]{1,0:T(8,128)(2,1)} %param.6) | data formatting | bytes 4194304 | tf_op args[0]
  11.3 29.9 %all_to_all.19 = bf16[128,4,2048]{0,2,1:T(8,128)(2,1)S(1)} all-to-all(bf16[128,4,2048]{0,2,1:T(8,128)(2,1)} %bitcast.16), channel_id=1, replica_groups=mesh['dp'=4,'vocab'=8] {'dp'}, dimensions={1} | all-to-all | bytes 4194304 | tf_op jit(solution)/shard_map/all_to_all | solution.py:19
  41.2 2.7 copy.9
  43.9 36.2 %fusion.7 = f32[512,12288]{1,0:T(8,128)} fusion(bf16[512,2048]{1,0:T(8,128)(2,1)} %bitcast.17, bf16[2048,12288]{1,0:T(8,128)(2,1)} %param.7), kind=kOutput, calls=%fused_computation.16 | convolution fusion | flops 25769803776 | bytes 77594624 | tf_op jit(solution)/shard_map/dot_general | solution.py:21
  80.1 0.0 copy-start.3
  80.1 0.0 copy-start.4
  80.1 0.0 reduce-scatter.2.cloned.1.call-update
  80.2 0.0 copy-start
  80.2 0.6 copy-done.3
  80.8 0.0 copy-done.4
  80.8 0.2 convolution_bitcast_fusion
  81.0 0.0 copy-start.1
  81.0 182.3 %reduce-scatter.2.cloned.1.call-done = f32[128,12288]{1,0:T(8,128)} async-done(((f32[512,12288]{1,0:T(8,128)}), f32[128,12288]{1,0:T(8,128)}) %reduce-scatter.2.cloned.1.call-update) | async-done | bytes 6291472 | tf_op jit(solution)/shard_map/reduce_scatter | solution.py:20
  263.4 3.1 reduce_max.9
  266.5 21.4 %pmax.7 = f32[128]{0:T(128)S(1)} all-reduce(f32[128]{0:T(128)S(1)} %reduce_max.9), channel_id=1, replica_groups=mesh['dp'=4,'vocab'=8] {'vocab'}, use_global_device_ids=true, to_apply=%region_2.0 | all-reduce | flops 128 | bytes 1024 | tf_op jit(solution)/shard_map/pmax | solution.py:30
  287.9 0.0 copy-done
  287.9 4.5 %exponential_reduce_fusion = (f32[128]{0:T(128)S(1)}, f32[128]{0:T(128)S(1)}) fusion(f32[128,12288]{1,0:T(8,128)} %reduce-scatter.2.cloned.1.call-done, f32[128]{0:T(128)S(1)} %reduce_max.9, s32[128]{0:T(128)S(1)} %copy-done, s32[12288]{0:T(1024)S(1)} %iota_add_fusion), kind=kLoop, calls=%fused_computation.1 | loop fusion | flops 7864064 | bytes 6342656 | tf_op jit(solution)/shard_map/reduce_sum | solution.py:27
  292.4 17.1 %all-reduce = (f32[128]{0:T(128)S(1)}, f32[128]{0:T(128)S(1)}) all-reduce(f32[128]{0:T(128)S(1)} %get-tuple-element.3, f32[128]{0:T(128)S(1)} %exponential_multiply_fusion), channel_id=1, replica_groups=mesh['dp'=4,'vocab'=8] {'vocab'}, use_global_device_ids=true, to_apply=%region_6.7 | all-reduce | flops 256 | bytes 2048 | tf_op jit(solution)/shard_map/psum | solution.py:31
  309.5 0.0 copy-start.2
  309.5 0.2 convolution_bitcast_fusion.1
  309.7 5.9 %all-reduce.1 = (f32[16]{0:T(128)S(1)}, f32[16]{0:T(128)S(1)}) all-reduce(f32[16]{0:T(128)S(1)} %convolution_bitcast_fusion.1, f32[16]{0:T(128)S(1)} %convolution_bitcast_fusion), channel_id=1, replica_groups=mesh['dp'=4,'vocab'=8] {'dp'}, use_global_device_ids=true, to_apply=%region_7.8 | all-reduce | flops 32 | bytes 256 | tf_op jit(solution)/shard_map/psum | solution.py:34
  315.7 0.0 copy-done.1
  315.7 0.5 maximum_divide_fusion
  316.2 0.0 copy-done.2
  (3 shorter events, 0.1 us)
Async XLA Ops:
  7.2 256.2 %reduce-scatter.2.cloned.1.call-start = ((), (), s32[]{:S(2)}) async-start(), calls=%async_computation.2 | async-start | bytes 31457280 | tf_op jit(solution)/shard_map/reduce_scatter | solution.py:20
  80.1 0.7 copy-start.3
  80.1 0.7 copy-start.4
  80.2 207.7 %copy-start = (s32[128]{0:T(128)S(1)}, s32[128]{0:T(128)}, u32[]{:S(2)}) copy-start(s32[128]{0:T(128)} %param.8) | copy-start | bytes 1540
  81.0 234.6 %copy-start.1 = (s32[16]{0:T(128)S(1)}, s32[16]{0:T(128)}, u32[]{:S(2)}) copy-start(s32[16]{0:T(128)} %param.11) | copy-start | bytes 196
  309.5 6.7 %copy-start.2 = (f32[128]{0:T(128)}, f32[128]{0:T(128)S(1)}, u32[]{:S(2)}) copy-start(f32[128]{0:T(128)S(1)} %add_subtract_fusion) | copy-start | bytes 1540
Sparse Core Ops, SparseCore 0:
  80.3 183.0 reduce-scatter.1
where the time goes:
time: 323 us
  waiting for transfers between devices  182 us (56%)
  blocking collectives  74.4 us (23%)
  matrix products  36.6 us (11%)
  between operations  14.1 us (4%)
  other arithmetic  8.19 us (3%)
  local copies, waits for them, and re-layouts  7.42 us (2%)
    reduce_scatter x1, waiting for transfers between devices, body(): lax.psum_scatter(jnp.dot(mixed, out_weight, preferred_element_type=jnp.fl...  182 us
    dot_general x1, matrix products, body(): jnp.dot(mixed, out_weight, preferred_element_type=jnp.float32)  36.2 us
    all_to_all x1, blocking collectives, body(): lax.all_to_all(hidden, 'dp', split_axis=1, concat_axis=0, tiled=True)  29.9 us
    pmax x1, blocking collectives, body(): largest = lax.pmax(local_max, 'vocab')  21.4 us
    psum x1, blocking collectives, body(): lax.psum((sumexp * jnp.exp(local_max - largest), picked), 'vocab')  17.1 us
  transfers between devices with their start and end apart: 1, of which 1 were waited for; matrix products, arithmetic and copies ran while one was open for 0% of the time, Pallas kernels for 0%

commit v1 on v0

v1 whole, which is shorter than its diff:
```python
import functools

import jax
import jax.numpy as jnp
from jax import lax
from jax.experimental import pallas as pl
from jax.experimental.pallas import tpu as pltpu
from jax.sharding import PartitionSpec as P

LANES = 128
TOP = 32767.0
TINY = 1e-30


def largest_tile(columns, most):
    tile = most
    while columns % tile:
        tile //= 2
    return tile


def kernel(dims, hidden, weight, targets, segment, mask, outside, loss_out, sample_out,
           hx, wbuf, ybuf, prt, qs, qr, ss, sr, scale_buf, tg, tcol, m_buf, s_buf, p_buf,
           stat, statr, samp, wsem, local_sem, hsem, csem_s, csem_r, fsem_s, fsem_r, tsem,
           ysem, prsem, qssem, qrsem, sssem, srsem, stsem, strsem, spsem, sprsem):
    dp, nv, rows, depth, tiles, tile, chunks = dims
    chips = dp // 2
    me, v = lax.axis_index("dp"), lax.axis_index("vocab")
    x, c = me // 2, me % 2
    partner = 2 * x + (1 - c)
    owner = 2 * lax.rem(x + 1, chips) + c
    source = 2 * lax.rem(x + chips - 1, chips) + c
    share = rows // chunks

    def remote(src, dst, send, recv, d, w):
        return pltpu.make_async_remote_copy(
            src_ref=src, dst_ref=dst, send_sem=send, recv_sem=recv,
            device_id=(d, w), device_id_type=pl.DeviceIdType.MESH)

    def wcopy(t, slot):
        return pltpu.make_async_copy(
            weight.at[:, pl.ds(pl.multiple_of(t * tile, tile), tile)], wbuf.at[slot], wsem.at[slot])

    def features(d):
        return pl.ds(pl.multiple_of(d * depth, depth), depth)

    def token_rows(d):
        return pl.ds(pl.multiple_of(d * rows, rows), rows)

    def chunk_rows(d, j):
        return pl.ds(pl.multiple_of(d * rows + j * share, share), share)

    wcopy(0, 0).start()
    own = pltpu.make_async_copy(hidden.at[:, features(me)], hx.at[token_rows(me)], local_sem)
    own.start()

    barrier = pltpu.get_barrier_semaphore()

    def greet(d, w):
        pl.semaphore_signal(barrier, inc=1, device_id=(d, w), device_id_type=pl.DeviceIdType.MESH)

    for o in range(1, dp):
        greet(lax.rem(me + o, dp), v)

    columns_met = [0, 1] if chips == 2 else [0, 1, chips - 1]

    def greet_vocab(o, carry):
        w = lax.rem(v + o, nv)
        for step in columns_met:
            greet(2 * lax.rem(x + step, chips) + c, w)
        return carry

    lax.fori_loop(1, nv, greet_vocab, 0)
    pl.semaphore_wait(barrier, dp - 1 + (nv - 1) * len(columns_met))

    to_partner = remote(hidden.at[:, features(partner)], hx.at[token_rows(me)],
                        hsem.at[0], hsem.at[1], partner, v)
    to_partner.start()
    targets_copy = remote(targets, tg, tsem.at[0], tsem.at[1], source, v)

    def crossing(step, e):
        d = 2 * lax.rem(x + step, chips) + e
        src = hidden.at[pl.ds(pl.multiple_of(v * share, share), share), features(d)]
        i = 2 * (step - 1) + e
        r = 2 * (chips - step - 1) + c
        return d, src, i, r

    def cross_start():
        for step in range(1, chips):
            for e in range(2):
                d, src, i, r = crossing(step, e)
                remote(src, hx.at[chunk_rows(me, v)], csem_s.at[i], csem_r.at[r], d, v).start()

    if chunks < nv:
        pl.when(v < chunks)(cross_start)
    else:
        cross_start()
    targets_copy.start()

    def spread_each(step, e, do):
        d = 2 * lax.rem(x + step, chips) + e
        i = 2 * (step - 1) + e

        def one(o, carry):
            w = lax.rem(v + o, nv)
            block = hx.at[chunk_rows(d, v)]
            copy = remote(block, block, fsem_s.at[i, o - 1], fsem_r.at[i, v], me, w)
            do(copy)
            return carry

        lax.fori_loop(1, nv, one, 0)

    def spread():
        for step in range(1, chips):
            for e in range(2):
                d = 2 * lax.rem(x + step, chips) + e
                i = 2 * (step - 1) + e
                block = hx.at[chunk_rows(d, v)]
                remote(block, block, csem_s.at[i], csem_r.at[i], d, v).wait_recv()
                spread_each(step, e, lambda copy: copy.start())

    def spread_wait(step):
        for e in range(2):
            d = 2 * lax.rem(x + step, chips) + e
            i = 2 * (step - 1) + e

            def one(j, carry):
                @pl.when(j != v)
                def _():
                    block = hx.at[chunk_rows(d, j)]
                    remote(block, block, fsem_s.at[i, 0], fsem_r.at[i, j], me, lax.rem(v + 1, nv)).wait_recv()
                return carry

            lax.fori_loop(0, chunks, one, 0)

    def dot_tile(group, slot, yslot):
        width = min(tile, 512)
        lhs_rows = pl.ds(pl.multiple_of(group * 2 * rows, 2 * rows), 2 * rows)

        def piece(j, carry):
            cols = pl.ds(pl.multiple_of(j * width, width), width)
            ybuf[yslot, :, cols] = jnp.dot(hx[lhs_rows, :], wbuf[slot, :, cols],
                                           preferred_element_type=jnp.float32)
            return carry

        lax.fori_loop(0, tile // width, piece, 0)

    def ycopy(s, t, yslot):
        half = pl.ds(pl.multiple_of((1 - c) * rows, rows), rows)
        return remote(ybuf.at[yslot, half], prt.at[s, t], ysem.at[yslot], prsem.at[s, t], partner, v)

    def qcopy(s, t):
        d = 2 * lax.rem(x + chips - s - 1 + chips, chips) + c
        return (remote(qs.at[s, t], qr.at[s, t], qssem.at[s, t], qrsem.at[s, t], d, v),
                remote(ss.at[s, t], sr.at[s, t], sssem.at[s, t], srsem.at[s, t], d, v))

    band = min(rows, 32)

    def total(s, t, yslot, b):
        mine = pl.ds(pl.multiple_of(c * rows + b * band, band), band)
        theirs = pl.ds(b * band, band)
        return ybuf[yslot, mine, :] + prt[s, t, theirs, :]

    def send_sums(s, t, yslot):
        ycopy(s, t, yslot).wait_recv()
        for b in range(rows // band):
            value = total(s, t, yslot, b)
            top = jnp.maximum(jnp.max(jnp.abs(value), axis=1, keepdims=True), TINY)
            code = jnp.round(value * (TOP / top)).astype(jnp.int32)
            qs[s, t, b * band:(b + 1) * band, :] = code.astype(jnp.int16)
            scale_buf[b * band:(b + 1) * band, :] = jnp.broadcast_to(top * (1.0 / TOP), (band, LANES))
        ss[s, t] = jnp.transpose(scale_buf[0:rows, :])[0:8, :]
        for copy in qcopy(s, t):
            copy.start()

    def finish(s, t, yslot):
        ycopy(s, t, yslot).wait_recv()
        for a in range(chips - 1):
            for copy in qcopy(a, t):
                copy.wait_recv()
            scale_buf[a * rows:(a + 1) * rows, :] = jnp.transpose(
                jnp.broadcast_to(sr[a, t, 0:1, :], (LANES, rows)))
        base = v * (tiles * tile) + t * tile
        lane = lax.broadcasted_iota(jnp.int32, (band, LANES), 1)
        for b in range(rows // band):
            here = slice(b * band, (b + 1) * band)
            value = total(s, t, yslot, b)
            parts = []
            for k in range(tile // LANES):
                part = value[:, k * LANES:(k + 1) * LANES]
                for a in range(chips - 1):
                    code = qr[a, t, here, k * LANES:(k + 1) * LANES].astype(jnp.int32)
                    part = part + code.astype(jnp.float32) * scale_buf[a * rows + b * band:a * rows + (b + 1) * band, :]
                parts.append(part)
            old = m_buf[here, :]
            new = functools.reduce(jnp.maximum, parts, old)
            acc = s_buf[here, :] * jnp.exp(old - new)
            picked = p_buf[here, :]
            wanted = tcol[here, :] - base
            for k, part in enumerate(parts):
                acc = acc + jnp.exp(part - new)
                picked = picked + jnp.where(lane + k * LANES == wanted, part, 0.0)
            m_buf[here, :] = new
            s_buf[here, :] = acc
            p_buf[here, :] = picked

    own.wait()
    to_partner.wait_recv()
    m_buf[...] = jnp.full(m_buf.shape, -jnp.inf, jnp.float32)
    s_buf[...] = jnp.zeros(s_buf.shape, jnp.float32)
    p_buf[...] = jnp.zeros(p_buf.shape, jnp.float32)

    for s in range(chips):
        group = lax.rem(x + chips - s, chips)
        last = s == chips - 1
        if s > 0:
            spread_wait(chips - s)
        if last:
            targets_copy.wait_recv()
            tcol[...] = jnp.transpose(jnp.broadcast_to(tg[0:1, :], (LANES, rows)))
        handle = finish if last else send_sums

        def step(t, carry, s=s, group=group, last=last, handle=handle):
            i = s * tiles + t
            slot = lax.rem(i, 2)
            wcopy(t, slot).wait()

            @pl.when(i + 1 < chips * tiles)
            def _():
                wcopy(lax.rem(t + 1, tiles), 1 - slot).start()

            @pl.when(i >= 2)
            def _():
                ycopy(s, t, slot).wait_send()

            dot_tile(group, slot, slot)
            ycopy(s, t, slot).start()

            @pl.when(t >= 1)
            def _():
                handle(s, t - 1, 1 - slot)

            if s == 0:
                @pl.when(t == min(1, tiles - 1))
                def _():
                    if chunks < nv:
                        pl.when(v < chunks)(spread)
                    else:
                        spread()
            return carry

        lax.fori_loop(0, tiles, step, 0)
        handle(s, tiles - 1, (s * tiles + tiles - 1) % 2)

    lane = lax.broadcasted_iota(jnp.int32, (rows, LANES), 1)
    peak = jnp.max(m_buf[...], axis=1, keepdims=True)
    mass = jnp.sum(s_buf[...] * jnp.exp(m_buf[...] - peak), axis=1, keepdims=True)
    hit = jnp.sum(p_buf[...], axis=1, keepdims=True)
    table = jnp.where(lane == 0, peak, jnp.where(lane == 1, mass, hit))
    stat[...] = jnp.transpose(table)[0:8, :]

    def stat_copy(w):
        return remote(stat, statr.at[v], stsem.at[w], strsem.at[v], owner, w)

    def stat_start(o, carry):
        stat_copy(lax.rem(v + o, nv)).start()
        return carry

    lax.fori_loop(0, nv, stat_start, 0)

    def stat_wait(w, carry):
        remote(stat, statr.at[w], stsem.at[w], strsem.at[w], owner, w).wait_recv()
        return carry

    lax.fori_loop(0, nv, stat_wait, 0)
    peak = statr[0, 0:1, :]
    for w in range(1, nv):
        peak = jnp.maximum(peak, statr[w, 0:1, :])
    mass = jnp.zeros_like(peak)
    hit = jnp.zeros_like(peak)
    for w in range(nv):
        mass = mass + statr[w, 1:2, :] * jnp.exp(statr[w, 0:1, :] - peak)
        hit = hit + statr[w, 2:3, :]
    loss = peak + jnp.log(mass) - hit
    loss_out[...] = loss

    samples = outside.shape[0]
    weights = mask[...].astype(jnp.float32)
    member = lax.broadcasted_iota(jnp.int32, (samples, rows), 0) == segment[...]
    sums = jnp.sum(jnp.where(member, loss * weights, 0.0), axis=1, keepdims=True)
    count = jnp.sum(jnp.where(member, weights, 0.0), axis=1, keepdims=True)
    wide = lax.broadcasted_iota(jnp.int32, (samples, LANES), 1)
    samp[me] = jnp.where(wide < LANES // 2, sums, count)

    def samp_copy(o, d):
        return remote(samp.at[d], samp.at[d], spsem.at[o - 1], sprsem.at[d], lax.rem(me + o, dp), v)

    for o in range(1, dp):
        samp_copy(o, me).start()
    for o in range(1, dp):
        samp_copy(o, lax.rem(me + o, dp)).wait_recv()
    both = samp[0]
    for d in range(1, dp):
        both = both + samp[d]
    sums = both[:, 0:1]
    count = both[:, LANES - 1:LANES]
    denom = jnp.maximum(count + outside[...].astype(jnp.float32), 1.0)
    sample_out[...] = sums / denom

    to_partner.wait_send()
    targets_copy.wait_send()

    def leave():
        for step in range(1, chips):
            for e in range(2):
                d, src, i, r = crossing(step, e)
                remote(src, hx.at[chunk_rows(me, v)], csem_s.at[i], csem_r.at[r], d, v).wait_send()
                spread_each(step, e, lambda copy: copy.wait_send())

    if chunks < nv:
        pl.when(v < chunks)(leave)
    else:
        leave()
    for k in range(min(2, chips * tiles)):
        ycopy(0, 0, k).wait_send()

    def sums_left(t, carry):
        for s in range(chips - 1):
            for copy in qcopy(s, t):
                copy.wait_send()
        return carry

    lax.fori_loop(0, tiles, sums_left, 0)

    def stat_left(w, carry):
        stat_copy(w).wait_send()
        return carry

    lax.fori_loop(0, nv, stat_left, 0)
    for o in range(1, dp):
        samp_copy(o, me).wait_send()


def solution(mesh):
    dp, nv = mesh.shape["dp"], mesh.shape["vocab"]

    def body(hidden, out_weight, targets, segment, loss_mask, outside_count):
        rows = hidden.shape[0]
        depth, columns = out_weight.shape
        samples = outside_count.shape[0]
        chips = dp // 2
        tile = largest_tile(columns, 1024)
        tiles = columns // tile
        chunks = min(nv, rows // 16)
        dims = (dp, nv, rows, depth, tiles, tile, chunks)
        sem = pltpu.SemaphoreType.DMA
        far = 2 * (chips - 1)
        vm = pl.BlockSpec(memory_space=pltpu.VMEM)
        hbm = pl.BlockSpec(memory_space=pl.ANY)
        loss, sample = pl.pallas_call(
            functools.partial(kernel, dims),
            out_shape=(jax.ShapeDtypeStruct((1, rows), jnp.float32),
                       jax.ShapeDtypeStruct((samples, LANES), jnp.float32)),
            in_specs=[hbm, hbm, vm, vm, vm, vm],
            out_specs=(vm, vm),
            scratch_shapes=[
                pltpu.VMEM((dp * rows, depth), jnp.bfloat16),
                pltpu.VMEM((2, depth, tile), jnp.bfloat16),
                pltpu.VMEM((2, 2 * rows, tile), jnp.float32),
                pltpu.VMEM((chips, tiles, rows, tile), jnp.float32),
                pltpu.VMEM((chips - 1, tiles, rows, tile), jnp.int16),
                pltpu.VMEM((chips - 1, tiles, rows, tile), jnp.int16),
                pltpu.VMEM((chips - 1, tiles, 8, rows), jnp.float32),
                pltpu.VMEM((chips - 1, tiles, 8, rows), jnp.float32),
                pltpu.VMEM(((chips - 1) * rows, LANES), jnp.float32),
                pltpu.VMEM((8, rows), jnp.int32),
                pltpu.VMEM((rows, LANES), jnp.int32),
                pltpu.VMEM((rows, LANES), jnp.float32),
                pltpu.VMEM((rows, LANES), jnp.float32),
                pltpu.VMEM((rows, LANES), jnp.float32),
                pltpu.VMEM((8, rows), jnp.float32),
                pltpu.VMEM((nv, 8, rows), jnp.float32),
                pltpu.VMEM((dp, samples, LANES), jnp.float32),
                sem((2,)), sem, sem((2,)), sem((far,)), sem((far,)),
                sem((far, nv - 1)), sem((far, chunks)), sem((2,)),
                sem((2,)), sem((chips, tiles)),
                sem((chips - 1, tiles)), sem((chips - 1, tiles)),
                sem((chips - 1, tiles)), sem((chips - 1, tiles)),
                sem((nv,)), sem((nv,)), sem((dp - 1,)), sem((dp,)),
            ],
            compiler_params=pltpu.CompilerParams(
                collective_id=0, has_side_effects=True, vmem_limit_bytes=60 * 1024 * 1024),
        )(hidden, out_weight,
          jnp.broadcast_to(targets[None, :], (8, rows)),
          segment[None, :], loss_mask[None, :],
          jnp.broadcast_to(outside_count[:, None], (samples, LANES)))
        return loss[0], sample[:, 0]

    return jax.shard_map(
        body,
        mesh=mesh,
        in_specs=(P("dp", None), P("dp", "vocab"), P("dp"), P("dp"), P("dp"), P()),
        out_specs=(P("dp"), P()),
        check_vma=False,
    )
```

time: 323 us -> 98.1 us (0.30)
  waiting for transfers between devices: 182 us -> 0 us
  Pallas kernels: 0 us -> 91.5 us
  blocking collectives: 74.4 us -> 0 us
  matrix products: 36.6 us -> 0 us
  between operations: 14.1 us -> 0.64 us
  other arithmetic: 8.19 us -> 0 us
    reduce_scatter x1 -> x0, waiting for transfers between devices: 182 us -> none  [body(): lax.psum_scatter(jnp.dot(mixed, out_weight, preferred_element_type=jnp.fl...]
    pallas_call x0 -> x1, Pallas kernels: none -> 91.5 us  [body(): pl.pallas_call(functools.partial(kernel, dims), out_shape=(jax.ShapeDtype...]
    dot_general x3 -> x0, matrix products: 36.6 us -> none  [the longest x1 36.2 us: body(): jnp.dot(mixed, out_weight, preferred_element_type=jnp.float32)]
    all_to_all x1 -> x0, blocking collectives: 29.9 us -> none  [body(): lax.all_to_all(hidden, 'dp', split_axis=1, concat_axis=0, tiled=True)]
    psum x2 -> x0, blocking collectives: 23.1 us -> none  [the longest x1 17.1 us: body(): lax.psum((sumexp * jnp.exp(local_max - largest), picked), 'vocab')]
    pmax x1 -> x0, blocking collectives: 21.4 us -> none  [body(): largest = lax.pmax(local_max, 'vocab')]
    reduce_sum x1 -> x0, other arithmetic: 4.48 us -> none  [body(): sumexp = jnp.sum(jnp.exp(logits - local_max[:, None]), axis=1)]
    unnamed x11 -> x1, local copies, waits for them, and re-layouts: 4.75 us -> 1.18 us
  transfers between devices with their start and end apart: 1 -> 0, of which waited for: 1 -> 0; matrix products, arithmetic and copies ran while one was open for 0% -> 0% of each run, Pallas kernels for 0% -> 0%
where the time goes in v1:
time: 98.1 us; the launch traced here: 97.2 us
  Pallas kernels  91.5 us (93%)
  local copies, waits for them, and re-layouts  5.06 us (5%)
    pallas_call x1, Pallas kernels, body(): pl.pallas_call(functools.partial(kernel, dims), out_shape=(jax.ShapeDtype...  91.5 us

profile of v1, /device:TPU:0, one launch (start us, length us, event | category | flops | bytes accessed | tf_op | source)
XLA Modules:
  0.0 97.2 jit_solution(14418061767474887395)
XLA Ops:
  0.6 1.2 %broadcast_in_dim.8.targets = s32[8,128]{1,0:T(8,128)} broadcast(s32[128]{0:T(128)} %param.8), dimensions={1} | broadcast | bytes 4608 | tf_op jit(solution)/shard_map/broadcast_in_dim | solution.py:394
  1.9 1.3 %broadcast_in_dim.21.outside = s32[16,128]{1,0:T(8,128)} broadcast(s32[16]{0:T(128)} %param.11), dimensions={0} | broadcast | bytes 8256 | tf_op jit(solution)/shard_map/broadcast_in_dim | solution.py:396
  3.2 91.5 %shard_map.77 = (f32[1,128]{1,0:T(1,128)}, f32[16,128]{1,0:T(8,128)}) custom-call(bf16[128,8192]{1,0:T(8,128)(2,1)} %hidden.1, bf16[2048,12288]{1,0:T(8,128)(2,1)} %weight.1, s32[8,128]{1,0:T(8,128)} %broadcast_in_dim.8.targets, s32[1,128]{1,0:T(1,128)} %bitcast.3, s32[1,128]{1,0:T(1,128)} %bitcast.4, s32[16,128]{1,0:T(8,128)} %broadcast_in_dim.21.outside), custom_call_target="tpu_custom_call" | custom-call | tf_op jit(solution)/shard_map/pallas_call | solution.py:360
  94.7 1.3 %slice_reduce_fusion = f32[16]{0:T(128)} fusion(f32[16,128]{1,0:T(8,128)} %get-tuple-element.5), kind=kLoop, calls=%fused_computation | loop fusion | bytes 128 | tf_op jit(solution)/shard_map/slice | solution.py:397
  96.1 1.2 %copy.9 = f32[128]{0:T(128)} copy(f32[128]{0:T(128)} %bitcast.5) | data formatting | bytes 1024
